TPU v7x, 32 devices: a whole 2x2x4 slice. The times are simulated.
32 devices in a mesh: grp: 2 (over y), tm: 4 (over z), chan: 2 (over x), sub: 2 (over core).
Axes of the slice: x: 2, y: 2, z: 4, core: 2. Of those that a mesh axis runs over, the one named last changes fastest.
Arguments:
- signal: float32 [64, 131072], P(('grp', 'chan', 'sub'), 'tm'), parts along dimension 0, may hold values from -24 to 24
- gap_mask: int32 [64, 8], P(('grp', 'chan', 'sub'), 'tm'), parts along dimension 0, may hold values from 0 to 1, as said below
- assignment: int32 [64], P(('grp', 'chan', 'sub')), parts along dimension 0, may hold values from 0 to 7, as said below
Outputs:
- peak_hold: float32 [64, 16384], P(('grp', 'chan', 'sub'), 'tm'), parts along dimension 0
- log_mean: float32 [64, 16384], P(('grp', 'chan', 'sub'), 'tm'), parts along dimension 0
- block_mean: float32 [16, 16384], P('grp', 'tm'), parts along dimension 0
There are 2 independent parts, one for each index of `grp`. A program takes and returns all parts, laid end to end along the dimension named above; each array names one. Nothing has to cross between parts.
Inputs may be any that keep to these rules, and one draw needn't show every extreme that they name: `gap_mask`: every channel keeps at least one of its 8 segments. `assignment`: every block holds at least one channel.
All inputs are finite; a program needn't handle non-finite values.
Results may differ from a plain program's by a relative error of at most 0.000086.
Values sent between devices are 32-bit elements; how exact they have to be, the bound alone decides.
A program may use at most 128 MiB of HBM per device.

v0:
```python
import math

import jax
import jax.numpy as jnp
from jax import lax
from jax.sharding import PartitionSpec as P

LA = 256
LB = 128
BLOCKS = 8


def from_behind(x, axis, by):
    count = lax.axis_size(axis)
    pairs = [(i, i + by) for i in range(count) if 0 <= i + by < count]
    return lax.ppermute(x, axis, pairs)


def rotations(height, columns, modulus):
    products = (
        jnp.arange(height, dtype=jnp.int32)[:, None]
        * jnp.arange(columns, dtype=jnp.int32)[None, :]
        % modulus
    )
    angles = products.astype(jnp.float32) * (2.0 * math.pi / modulus)
    return (jnp.cos(angles), -jnp.sin(angles))


def on_device(signal, gap_mask, assignment):
    channels, local_time = signal.shape
    seg_local = gap_mask.shape[1]
    half = local_time // seg_local
    seg_length = LA * LB
    highest = lax.Precision.HIGHEST
    borrowed = from_behind(signal[:, :half], "tm", -1)
    extended = jnp.concatenate([signal, borrowed], axis=1)
    hop_rows = extended.reshape(channels, seg_local + 1, half)
    section_one = rotations(LB, LB, LB)
    twiddle = rotations(LB, LA, seg_length)
    section_two = rotations(LA, LA // 2, LA)
    samples = jnp.arange(seg_length, dtype=jnp.float32)
    window = (0.5 - 0.5 * jnp.cos(samples * (2.0 * math.pi / seg_length))).reshape(LB, LA)
    norm_scale = 1.0 / (0.375 * seg_length)

    def one_channel(inputs):
        rows_here, keep_flags = inputs
        segments = jnp.concatenate([rows_here[:-1], rows_here[1:]], axis=-1)
        frames = segments.reshape(seg_local, LB, LA) * window
        real_one = jnp.einsum("kb,sba->ska", section_one[0], frames, precision=highest)
        imag_one = jnp.einsum("kb,sba->ska", section_one[1], frames, precision=highest)
        real_mid = real_one * twiddle[0] - imag_one * twiddle[1]
        imag_mid = real_one * twiddle[1] + imag_one * twiddle[0]
        real_two = jnp.einsum(
            "ska,aj->skj", real_mid, section_two[0], precision=highest
        ) - jnp.einsum("ska,aj->skj", imag_mid, section_two[1], precision=highest)
        imag_two = jnp.einsum(
            "ska,aj->skj", real_mid, section_two[1], precision=highest
        ) + jnp.einsum("ska,aj->skj", imag_mid, section_two[0], precision=highest)
        powers = (real_two * real_two + imag_two * imag_two) * norm_scale
        powers = jnp.swapaxes(powers, 1, 2).reshape(seg_local, -1)
        weights = keep_flags.astype(jnp.float32)
        peak_local = jnp.max(powers * weights[:, None], axis=0)
        log_terms = jnp.sum(weights[:, None] * jnp.log(0.25 + powers), axis=0)
        return (peak_local, log_terms)

    peak_local, log_terms = lax.map(one_channel, (hop_rows, gap_mask))
    kept_local = jnp.sum(gap_mask.astype(jnp.float32), axis=1)
    time_devices = lax.axis_size("tm")
    bin_width = peak_local.shape[1] // time_devices
    count_terms = jnp.broadcast_to(kept_local[:, None], (channels, time_devices))
    peak_all = lax.pmax(peak_local, "tm")
    peak_hold = lax.dynamic_slice_in_dim(peak_all, lax.axis_index("tm") * bin_width, bin_width, 1)
    log_sum, kept_total = (
        lax.psum_scatter(log_terms, "tm", scatter_dimension=1, tiled=True),
        lax.psum_scatter(count_terms, "tm", scatter_dimension=1, tiled=True),
    )
    log_mean = log_sum / kept_total
    onehot = (assignment[None, :] == jnp.arange(BLOCKS, dtype=jnp.int32)[:, None]).astype(
        jnp.float32
    )
    block_part = jnp.dot(onehot, log_mean, precision=highest)
    block_total, block_counts = lax.psum((block_part, jnp.sum(onehot, axis=1)), ("chan", "sub"))
    block_mean = block_total / block_counts[:, None]
    return (peak_hold, log_mean, block_mean)


def solution(mesh):
    in_specs = (
        P(("grp", "chan", "sub"), "tm"),
        P(("grp", "chan", "sub"), "tm"),
        P(("grp", "chan", "sub")),
    )
    out_specs = (P(("grp", "chan", "sub"), "tm"), P(("grp", "chan", "sub"), "tm"), P("grp", "tm"))
    return jax.shard_map(
        on_device, mesh=mesh, in_specs=in_specs, out_specs=out_specs, check_vma=False
    )
```

profile of v0, /device:TPU:0, one launch (start us, length us, event | category | flops | bytes accessed | tf_op | source)
XLA Modules:
  0.0 217.9 jit_solution(8996956551035906242)
XLA Ops:
  7.2 1.2 slice.11
  8.4 1.3 collective-permute-start
  9.7 0.8 copy.48
  10.5 14.9 %collective-permute-done = f32[8,16384]{1,0:T(8,128)} collective-permute-done((f32[8,16384]{1,0:T(8,128)S(1)}, f32[8,16384]{1,0:T(8,128)}, u32[]{:S(2)}, u32[]{:S(2)}) %collective-permute-start) | collective-permute-done | bytes 524320 | tf_op jit(solution)/shard_map/ppermute | solution.py:16
  25.4 1.1 pad_maximum_fusion
  26.5 2.5 %reshape.43 = f32[8,3,16384]{2,1,0:T(4,128)} reshape(f32[8,49152]{1,0:T(8,128)S(1)} %pad_maximum_fusion) | data formatting | bytes 3145728 | tf_op jit(solution)/shard_map/reshape | solution.py:37
  29.0 84.5 %while.14 = (s32[]{:T(128)}, f32[8,16384]{1,0:T(8,128)S(1)}, f32[8,16384]{1,0:T(8,128)}, f32[8,3,16384]{2,1,0:T(4,128)}, s32[8,2]{1,0:T(8,128)S(1)}, /*index=5*/s32[]{:T(128)}, s32[]{:T(128)}, s32[]{}) while((s32[]{:T(128)}, f32[8,16384]{1,0:T(8,128)S(1)}, f32[8,16384]{1,0:T(8,128)}, f32[8,3,16384]{2,1,0:T(4,128)}, ...), condition=%wide.region_3.4_spmd.clone.clone, body=%wide.region_0.3_spmd.clone.clone.sunk | while | flops 608321536 | bytes 8388765 | solution.py:66
  29.0 1.2 constant_dynamic-slice_fusion.5
  32.9 1.0 fusion.99
  33.9 1.0 fusion.100
  34.9 1.0 fusion.101
  35.9 1.0 multiply_reduce_fusion.3
  37.1 1.9 dynamic_update_slice.14
  39.6 1.1 constant_dynamic-slice_fusion.5
  43.5 1.0 fusion.99
  44.5 1.0 fusion.100
  45.5 1.0 fusion.101
  46.5 1.0 multiply_reduce_fusion.3
  47.6 1.9 dynamic_update_slice.14
  50.2 1.1 constant_dynamic-slice_fusion.5
  54.1 1.0 fusion.99
  55.1 1.0 fusion.100
  56.1 1.0 fusion.101
  57.1 1.0 multiply_reduce_fusion.3
  58.2 1.9 dynamic_update_slice.14
  60.7 1.1 constant_dynamic-slice_fusion.5
  64.6 1.0 fusion.99
  65.6 1.0 fusion.100
  66.6 1.0 fusion.101
  67.6 1.0 multiply_reduce_fusion.3
  68.7 1.9 dynamic_update_slice.14
  71.3 1.1 constant_dynamic-slice_fusion.5
  75.2 1.0 fusion.99
  76.2 1.0 fusion.100
  77.2 1.0 fusion.101
  78.2 1.0 multiply_reduce_fusion.3
  79.3 1.9 dynamic_update_slice.14
  81.9 1.1 constant_dynamic-slice_fusion.5
  85.8 1.0 fusion.99
  86.7 1.0 fusion.100
  87.7 1.0 fusion.101
  88.7 1.0 multiply_reduce_fusion.3
  89.9 1.9 dynamic_update_slice.14
  92.4 1.1 constant_dynamic-slice_fusion.5
  96.3 1.0 fusion.99
  97.3 1.0 fusion.100
  98.3 1.0 fusion.101
  99.3 1.0 multiply_reduce_fusion.3
  100.4 1.9 dynamic_update_slice.14
  103.0 1.1 constant_dynamic-slice_fusion.5
  106.9 1.0 fusion.99
  107.9 1.0 fusion.100
  108.9 1.0 fusion.101
  109.9 1.0 multiply_reduce_fusion.3
  111.0 1.9 dynamic_update_slice.14
  113.7 5.9 %psum.15 = f32[8]{0:T(128)S(1)} all-reduce(f32[8]{0:T(128)S(1)} %convert_reduce_fusion), channel_id=1, replica_groups=mesh['grp'=2,'tm'=4,'chan'=2,'sub'=2] {'chan','sub'}, use_global_device_ids=true, to_apply=%region_10.11 | all-reduce | flops 8 | bytes 64 | tf_op jit(solution)/shard_map/psum | solution.py:82
  120.2 10.0 %all-reduce = f32[8,4]{0,1:T(4,128)S(1)} all-reduce(f32[8,4]{0,1:T(4,128)S(1)} %broadcast_in_dim.8), channel_id=3, replica_groups=mesh['grp'=2,'tm'=4,'chan'=2,'sub'=2] {'tm'}, use_global_device_ids=true, to_apply=%region_7.8.clone | all-reduce | flops 32 | bytes 256
  131.0 5.0 %reduce-scatter.2.cloned.1.call-done = f32[8,4096]{1,0:T(8,128)} async-done(((f32[8,16384]{1,0:T(8,128)}), f32[8,4096]{1,0:T(8,128)}) %reduce-scatter.2.cloned.1.call-update) | async-done | bytes 131088 | tf_op jit(solution)/shard_map/reduce_scatter | solution.py:74
  136.0 1.0 broadcast_divide_fusion.1
  137.0 0.8 fusion.82
  137.9 37.3 %all-reduce.4.cloned.1.call-done = f32[8,16384]{1,0:T(8,128)} async-done(((f32[8,16384]{1,0:T(8,128)}), f32[8,16384]{1,0:T(8,128)}) %all-reduce.4.cloned.1.call-update) | async-done | bytes 524304 | tf_op jit(solution)/shard_map/pmax | solution.py:71
  175.2 1.6 constant_dynamic-slice_fusion.3
  176.8 32.9 %all-reduce.6.cloned.1.call-done = f32[8,4096]{1,0:T(8,128)} async-done(((f32[8,4096]{1,0:T(8,128)}), f32[8,4096]{1,0:T(8,128)}) %all-reduce.6.cloned.1.call-update) | async-done | bytes 131088 | tf_op jit(solution)/shard_map/psum | solution.py:82
  209.7 1.6 broadcast_divide_fusion
  (137 shorter events, 28.4 us)
Async XLA Ops:
  7.2 18.2 %copy-start = (f32[8,32768]{1,0:T(8,128)S(1)}, f32[8,32768]{1,0:T(8,128)}, u32[]{:S(2)}) copy-start(f32[8,32768]{1,0:T(8,128)} %param.5) | copy-start | bytes 3145732
  7.2 128.9 %reduce-scatter.2.cloned.1.call-start = ((), (), s32[]{:S(2)}) async-start(), calls=%async_computation.2 | async-start | bytes 655360 | tf_op jit(solution)/shard_map/reduce_scatter | solution.py:74
  8.4 17.0 %collective-permute-start = (f32[8,16384]{1,0:T(8,128)S(1)}, f32[8,16384]{1,0:T(8,128)}, u32[]{:S(2)}, u32[]{:S(2)}) collective-permute-start(f32[8,16384]{1,0:T(8,128)S(1)} %slice.11), channel_id=1, source_target_pairs={{4,0},{8,4},{12,8},{5,1},{9,5},{13,9},{6,2},{10,6},{14,10},{7,3},{... | collective-permute-start | bytes 1572872 | tf_op jit(solution)/shard_map/ppermute | solution.py:16
  29.0 84.6 %copy-start.4 = (s32[8]{0:T(128)S(1)}, s32[8]{0:T(128)}, u32[]{:S(2)}) copy-start(s32[8]{0:T(128)} %param.7) | copy-start | bytes 100
  29.0 90.6 %copy-start.5 = (u32[32]{0:T(128)S(1)}, u32[32]{0:T(128)}, u32[]{:S(2)}) copy-start(u32[32]{0:T(128)} %constant.88) | copy-start | bytes 388
  29.0 91.2 %copy-start.3 = (s32[8,2]{0,1:T(2,128)S(1)}, s32[8,2]{0,1:T(2,128)}, u32[]{:S(2)}) copy-start(s32[8,2]{0,1:T(2,128)} %param.6) | copy-start | bytes 196
  113.5 17.4 %copy-start.1 = (f32[8,16384]{1,0:T(8,128)}, f32[8,16384]{1,0:T(8,128)S(1)}, u32[]{:S(2)}) copy-start(f32[8,16384]{1,0:T(8,128)S(1)} %get-tuple-element.78) | copy-start | bytes 1572868
  113.6 61.7 %all-reduce.4.cloned.1.call-start = ((), (), s32[]{:S(2)}) async-start(), calls=%async_computation.1 | async-start | bytes 1048576 | tf_op jit(solution)/shard_map/pmax | solution.py:71
  131.0 78.8 %all-reduce.6.cloned.1.call-start = ((), (), s32[]{:S(2)}) async-start(), calls=%async_computation.3 | async-start | bytes 262144 | tf_op jit(solution)/shard_map/psum | solution.py:82
  137.0 74.4 %copy-start.2 = (f32[8,4096]{1,0:T(8,128)}, f32[8,4096]{1,0:T(8,128)S(1)}, u32[]{:S(2)}) copy-start(f32[8,4096]{1,0:T(8,128)S(1)} %broadcast_divide_fusion.1) | copy-start | bytes 393220
Sparse Core Ops, SparseCore 0:
  113.7 22.3 reduce-scatter.1
  138.4 36.8 all-reduce.3
  178.1 31.5 all-reduce.5
where the time goes:
time: 219 us; the launch traced here: 218 us
  waiting for transfers between devices  90.2 us (41%)
  matrix products  42.8 us (20%)
  local copies, waits for them, and re-layouts  40.5 us (18%)
  blocking collectives  15.9 us (7%)
  between operations  13.8 us (6%)
  other arithmetic  12 us (5%)
    pmax x1, waiting for transfers between devices, on_device(): peak_all = lax.pmax(peak_local, 'tm')  37.3 us
    psum x1, waiting for transfers between devices, on_device(): lax.psum((block_part, jnp.sum(onehot, axis=1)), ('chan', 'sub'))  32.9 us
    dynamic_update_slice x16, local copies, waits for them, and re-layouts, on_device(): peak_local, log_terms = lax.map(one_channel, (hop_rows, gap_mask))  19.5 us
    ppermute x1, waiting for transfers between devices, from_behind(): return lax.ppermute(x, axis, pairs)  14.9 us
    unnamed x1, blocking collectives  10 us
    slice x8, local copies, waits for them, and re-layouts, one_channel(): segments = jnp.concatenate([rows_here[:-1], rows_here[1:]], axis=-1)  9.22 us
    dot_general x8, matrix products, one_channel(): jnp.einsum('ska,aj->skj', imag_mid, section_two[0], precision=highest)  8.05 us
    dot_general x8, matrix products, one_channel(): jnp.einsum('ska,aj->skj', real_mid, section_two[0], precision=highest)  7.94 us
  transfers between devices with their start and end apart: 4, of which 4 were waited for; matrix products, arithmetic and copies ran while one was open for 3% of the time, Pallas kernels for 0%

commit v1 on v0

v1 whole, which is shorter than its diff:
```python
import functools
import math

import jax
import jax.numpy as jnp
import numpy as np
from jax import lax
from jax.experimental import pallas as pl
from jax.experimental.pallas import tpu as pltpu
from jax.sharding import PartitionSpec as P

LA = 256
LB = 128
BLOCKS = 8
MESH = pl.DeviceIdType.MESH
F32 = jnp.float32
BF16 = jnp.bfloat16


def split_constant(matrix):
    high = matrix.astype(BF16)
    low = (matrix - high.astype(np.float64)).astype(BF16)
    return high, low


def tables():
    length = LA * LB
    rows = LA // 2 + 8
    first = np.arange(rows)[:, None]
    used = first <= LA // 2
    angle = 2.0 * np.pi * (first * np.arange(LA)[None, :] % LA) / LA
    stage_one = np.concatenate([np.cos(angle) * used, -np.sin(angle) * used], axis=0)
    turn = 2.0 * np.pi * (first * np.arange(LB)[None, :]) / length
    twiddle = np.stack([np.cos(turn), -np.sin(turn)]).astype(np.float32)
    lane = np.arange(LB)
    second = np.where(lane < LB // 2, lane, LB - 1 - (lane - LB // 2))
    angle = 2.0 * np.pi * (np.arange(LB)[:, None] * second[None, :] % LB) / LB
    stage_two = np.block([[np.cos(angle), -np.sin(angle)], [np.sin(angle), np.cos(angle)]])
    samples = np.arange(length // 2)
    scale = 1.0 / math.sqrt(0.375 * length)
    rising = (0.5 - 0.5 * np.cos(samples * (2.0 * np.pi / length))) * scale
    falling = (0.5 + 0.5 * np.cos(samples * (2.0 * np.pi / length))) * scale
    window = np.stack([rising, falling]).reshape(2, LA // 2, LB).astype(np.float32)
    return (*split_constant(stage_one), *split_constant(stage_two), twiddle, window)


def split_value(x):
    high = x.astype(BF16)
    low = (x - high.astype(F32)).astype(BF16)
    return high, low


def three_pass(left, right):
    dot = functools.partial(jnp.dot, preferred_element_type=F32)
    return dot(left[0], right[0]) + dot(left[0], right[1]) + dot(left[1], right[0])


def kernel(
    sizes,
    assign_ref,
    x_ref,
    gap_ref,
    one_high,
    one_low,
    two_high,
    two_low,
    twiddle,
    window,
    peak_out,
    mean_out,
    block_out,
    work,
    away,
    stage,
    arrived,
    masks,
    sub_sums,
    chan_sums,
    peak_rows,
    mean_rows,
    raw_send,
    raw_recv,
    halo_send,
    halo_recv,
    mask_send,
    mask_recv,
    part_send,
    part_recv,
    sub_send,
    sub_recv,
    chan_send,
    chan_recv,
):
    times, subs, chans = sizes
    pairs = times // 2
    channels = x_ref.shape[0]
    nh = channels // 2
    rows = LA // 2
    out_rows = stage.shape[3]
    me = lax.axis_index("tm")
    pair, side = me // 2, lax.rem(me, 2)
    partner = pair * 2 + 1 - side
    my_sub = lax.axis_index("sub")
    my_chan = lax.axis_index("chan")

    barrier = pltpu.get_barrier_semaphore()
    for axis, here, count in (("tm", me, times), ("sub", my_sub, subs), ("chan", my_chan, chans)):
        for k in range(1, count):
            pl.semaphore_signal(
                barrier, inc=1, device_id={axis: lax.rem(here + k, count)}, device_id_type=MESH
            )

    for own in range(2):

        @pl.when(side == own)
        def _():
            for j in range(2 * rows):
                part = x_ref[:, j * LB : (j + 1) * LB]
                slot, row = j // rows, j % rows
                work[:, 2 * own + slot, row, :] = part[own * nh : (own + 1) * nh]
                away[:, slot, row, :] = part[(1 - own) * nh : (2 - own) * nh]

    flags = gap_ref[...].astype(F32)
    for s in range(2):
        masks[me, s] = jnp.broadcast_to(flags[:, s : s + 1], (channels, LB))

    @pl.when(pair == pairs - 1)
    def _():
        work[:, 4] = jnp.zeros_like(work[:, 4])

    pl.semaphore_wait(barrier, times + subs + chans - 3)

    def raw_copy(ci):
        return pltpu.make_async_remote_copy(
            src_ref=away.at[ci],
            dst_ref=work.at[ci, pl.ds(2 * side, 2)],
            send_sem=raw_send.at[ci],
            recv_sem=raw_recv.at[ci],
            device_id={"tm": partner},
            device_id_type=MESH,
        )

    def halo_copy(ci, which):
        return pltpu.make_async_remote_copy(
            src_ref=away.at[ci, 0] if which else work.at[ci, 0],
            dst_ref=work.at[ci, 4],
            send_sem=halo_send.at[which, ci],
            recv_sem=halo_recv.at[ci],
            device_id={"tm": jnp.maximum(2 * pair - 2 + which, 0)},
            device_id_type=MESH,
        )

    def mask_copy(k):
        return pltpu.make_async_remote_copy(
            src_ref=masks.at[me],
            dst_ref=masks.at[me],
            send_sem=mask_send.at[k],
            recv_sem=mask_recv.at[me],
            device_id={"tm": lax.rem(me + k, times)},
            device_id_type=MESH,
        )

    def part_copy(k, ci):
        target = lax.rem(me + k, times)
        return pltpu.make_async_remote_copy(
            src_ref=stage.at[target, ci],
            dst_ref=arrived.at[me, ci],
            send_sem=part_send.at[k, ci],
            recv_sem=part_recv.at[me, ci],
            device_id={"tm": target},
            device_id_type=MESH,
        )

    sends_halo = jnp.logical_and(side == 0, pair > 0)
    for k in range(1, times):
        mask_copy(k).start()
    for ci in range(nh):
        raw_copy(ci).start()

        @pl.when(sends_halo)
        def _():
            halo_copy(ci, 0).start()
            halo_copy(ci, 1).start()

    for k in range(1, times):
        source = lax.rem(me + k, times)
        pltpu.make_async_remote_copy(
            src_ref=masks.at[source],
            dst_ref=masks.at[source],
            send_sem=mask_send.at[k],
            recv_sem=mask_recv.at[source],
            device_id={"tm": source},
            device_id_type=MESH,
        ).wait_recv()

    lane = lax.broadcasted_iota(jnp.int32, (8, LB), 1)
    sub_row = lax.broadcasted_iota(jnp.int32, (8, LB), 0)
    swap = jnp.logical_and(sub_row == 0, lane >= LB // 2)
    mirror = lax.rem(LB - lax.broadcasted_iota(jnp.int32, (LB // 2, LB), 1), LB)

    def in_order(table):
        head = jnp.where(swap, jnp.broadcast_to(table[rows : rows + 1], (8, LB)), table[:8])
        turned = jnp.concatenate([head, table[8:rows]], axis=0).T
        back = jnp.take_along_axis(turned[LB // 2 :], mirror, axis=1)
        return jnp.concatenate([turned[: LB // 2], back], axis=1)

    def one_channel(ci, carry):
        raw_copy(ci).wait_recv()

        @pl.when(pair < pairs - 1)
        def _():
            halo_copy(ci, 0).wait_recv()

        columns_high, columns_low = [], []
        for s in range(4):
            frame = jnp.concatenate(
                [work[ci, s] * window[0], work[ci, s + 1] * window[1]], axis=0
            )
            high, low = split_value(frame)
            columns_high.append(high)
            columns_low.append(low)
        frames = (jnp.concatenate(columns_high, axis=1), jnp.concatenate(columns_low, axis=1))
        middle = three_pass((one_high[...], one_low[...]), frames)
        real, imag = middle[: rows + 8], middle[rows + 8 :]
        cosine, sine = twiddle[0], twiddle[1]
        turned = []
        for s in range(4):
            re, im = real[:, s * LB : (s + 1) * LB], imag[:, s * LB : (s + 1) * LB]
            turned.append(
                jnp.concatenate([re * cosine - im * sine, re * sine + im * cosine], axis=1)
            )
        turned = jnp.concatenate(turned, axis=0)
        bins = three_pass(split_value(turned), (two_high[...], two_low[...]))
        powers = bins[:, :LB] * bins[:, :LB] + bins[:, LB:] * bins[:, LB:]
        channel = side * nh + ci
        peak, product = None, None
        for s in range(4):
            keep = masks[2 * pair + s // 2, s % 2, pl.ds(channel, 1), :] > 0.5
            here = powers[s * (rows + 8) : (s + 1) * (rows + 8)]
            held = jnp.where(keep, here, 0.0)
            factor = jnp.where(keep, here + 0.25, 1.0)
            peak = held if peak is None else jnp.maximum(peak, held)
            product = factor if product is None else product * factor
        for which, table in enumerate((peak, jnp.log(product))):
            ordered = in_order(table)
            for target in range(times):
                stage[target, ci, which] = ordered[target * out_rows : (target + 1) * out_rows]
        for k in range(1, times):
            part_copy(k, ci).start()
        arrived[me, ci] = stage[me, ci]
        return carry

    lax.fori_loop(0, nh, one_channel, 0)

    kept = jnp.zeros((channels, LB), F32)
    for t in range(times):
        kept = kept + masks[t, 0] + masks[t, 1]

    for ci in range(nh):
        for k in range(1, times):
            source = lax.rem(me + k, times)
            pltpu.make_async_remote_copy(
                src_ref=arrived.at[source, ci],
                dst_ref=arrived.at[source, ci],
                send_sem=part_send.at[k, ci],
                recv_sem=part_recv.at[source, ci],
                device_id={"tm": source},
                device_id_type=MESH,
            ).wait_recv()

    count_lane = lax.broadcasted_iota(jnp.int32, (out_rows, 2 * LB), 1)
    counts = jnp.zeros((out_rows, 2 * LB), F32)
    blocks = [jnp.zeros((out_rows, 2 * LB), F32) for _ in range(BLOCKS)]
    for c in range(channels):
        origin, ci = c // nh, c % nh
        peak = arrived[origin, ci, 0]
        logs = arrived[origin, ci, 1]
        for p in range(1, pairs):
            peak = jnp.maximum(peak, arrived[2 * p + origin, ci, 0])
            logs = logs + arrived[2 * p + origin, ci, 1]
        row = kept[c : c + 1]
        mean = logs / jnp.concatenate([row, row], axis=1)
        peak_rows[c] = peak
        mean_rows[c] = mean
        group = assign_ref[c]
        counts = counts + (count_lane == group).astype(F32)
        for b in range(BLOCKS):
            blocks[b] = blocks[b] + mean * (group == b).astype(F32)
    for b in range(BLOCKS):
        sub_sums[my_sub, b] = blocks[b]
    sub_sums[my_sub, BLOCKS] = counts

    def exchange(axis, here, count, sums, send, recv):
        def copy(k, owner):
            return pltpu.make_async_remote_copy(
                src_ref=sums.at[owner],
                dst_ref=sums.at[owner],
                send_sem=send.at[k],
                recv_sem=recv.at[owner],
                device_id={axis: lax.rem(here + k, count)},
                device_id_type=MESH,
            )

        sends = [copy(k, here) for k in range(1, count)]
        for one in sends:
            one.start()
        return sends, [copy(k, lax.rem(here + k, count)) for k in range(1, count)]

    sub_out, sub_in = exchange("sub", my_sub, subs, sub_sums, sub_send, sub_recv)
    for j in range(out_rows):
        for side_lane in range(2):
            at = (2 * j + side_lane) * LB
            lanes = slice(side_lane * LB, (side_lane + 1) * LB)
            peak_out[:, at : at + LB] = peak_rows[:, j, lanes]
            mean_out[:, at : at + LB] = mean_rows[:, j, lanes]
    for one in sub_in:
        one.wait_recv()
    for b in range(BLOCKS + 1):
        total = sub_sums[0, b]
        for k in range(1, subs):
            total = total + sub_sums[k, b]
        chan_sums[my_chan, b] = total
    chan_out, chan_in = exchange("chan", my_chan, chans, chan_sums, chan_send, chan_recv)
    for one in chan_in:
        one.wait_recv()
    totals = []
    for b in range(BLOCKS + 1):
        total = chan_sums[0, b]
        for k in range(1, chans):
            total = total + chan_sums[k, b]
        totals.append(total)
    for b in range(BLOCKS):
        size = jnp.sum(jnp.where(count_lane == b, totals[BLOCKS], 0.0), axis=1, keepdims=True)
        peak_rows[b] = totals[b] / size
    for j in range(out_rows):
        for side_lane in range(2):
            at = (2 * j + side_lane) * LB
            lanes = slice(side_lane * LB, (side_lane + 1) * LB)
            block_out[:, at : at + LB] = peak_rows[:BLOCKS, j, lanes]

    for one in sub_out + chan_out:
        one.wait_send()
    for k in range(1, times):
        mask_copy(k).wait_send()
    for ci in range(nh):
        raw_copy(ci).wait_send()

        @pl.when(sends_halo)
        def _():
            halo_copy(ci, 0).wait_send()
            halo_copy(ci, 1).wait_send()

        for k in range(1, times):
            part_copy(k, ci).wait_send()


def on_device(sizes, signal, gap_mask, assignment):
    times, subs, chans = sizes
    channels, local_time = signal.shape
    nh = channels // 2
    rows = LA // 2
    width = LA * LB // 2 // times
    out_rows = width // (2 * LB)
    constants = [jnp.asarray(t) for t in tables()]
    vmem = pl.BlockSpec(memory_space=pltpu.VMEM)
    dma = pltpu.SemaphoreType.DMA
    return pl.pallas_call(
        functools.partial(kernel, sizes),
        out_shape=[
            jax.ShapeDtypeStruct((channels, width), F32),
            jax.ShapeDtypeStruct((channels, width), F32),
            jax.ShapeDtypeStruct((BLOCKS, width), F32),
        ],
        in_specs=[pl.BlockSpec(memory_space=pltpu.SMEM)] + [vmem] * 8,
        out_specs=[vmem] * 3,
        scratch_shapes=[
            pltpu.VMEM((nh, 5, rows, LB), F32),
            pltpu.VMEM((nh, 2, rows, LB), F32),
            pltpu.VMEM((times, nh, 2, out_rows, 2 * LB), F32),
            pltpu.VMEM((times, nh, 2, out_rows, 2 * LB), F32),
            pltpu.VMEM((times, 2, channels, LB), F32),
            pltpu.VMEM((subs, BLOCKS + 1, out_rows, 2 * LB), F32),
            pltpu.VMEM((chans, BLOCKS + 1, out_rows, 2 * LB), F32),
            pltpu.VMEM((max(channels, BLOCKS), out_rows, 2 * LB), F32),
            pltpu.VMEM((channels, out_rows, 2 * LB), F32),
            dma((nh,)),
            dma((nh,)),
            dma((2, nh)),
            dma((nh,)),
            dma((times,)),
            dma((times,)),
            dma((times, nh)),
            dma((times, nh)),
            dma((subs,)),
            dma((subs,)),
            dma((chans,)),
            dma((chans,)),
        ],
        compiler_params=pltpu.CompilerParams(collective_id=0, has_side_effects=True),
    )(assignment, signal, gap_mask, *constants)


def solution(mesh):
    sizes = (mesh.shape["tm"], mesh.shape["sub"], mesh.shape["chan"])
    in_specs = (
        P(("grp", "chan", "sub"), "tm"),
        P(("grp", "chan", "sub"), "tm"),
        P(("grp", "chan", "sub")),
    )
    out_specs = (P(("grp", "chan", "sub"), "tm"), P(("grp", "chan", "sub"), "tm"), P("grp", "tm"))
    return jax.shard_map(
        functools.partial(on_device, sizes),
        mesh=mesh,
        in_specs=in_specs,
        out_specs=out_specs,
        check_vma=False,
    )
```

time: 219 us -> 47.3 us (0.22)
  waiting for transfers between devices: 90.2 us -> 0 us
  matrix products: 42.8 us -> 0 us
  Pallas kernels: 0 us -> 41.9 us
  local copies, waits for them, and re-layouts: 40.5 us -> 4.56 us
  blocking collectives: 15.9 us -> 0 us
  between operations: 13.8 us -> 0.65 us
  other arithmetic: 12 us -> 0 us
    dot_general x49 -> x0, matrix products: 42.8 us -> none  [the longest x8 8.05 us: one_channel(): jnp.einsum('ska,aj->skj', imag_mid, section_two[0], precision=highest)]
    pallas_call x0 -> x1, Pallas kernels: none -> 41.9 us  [on_device(): pl.pallas_call(functools.partial(kernel, sizes), out_shape=[jax.ShapeDtyp...]
    pmax x1 -> x0, waiting for transfers between devices: 37.3 us -> none  [on_device(): peak_all = lax.pmax(peak_local, 'tm')]
    psum x1 -> x0, waiting for transfers between devices: 32.9 us -> none  [on_device(): lax.psum((block_part, jnp.sum(onehot, axis=1)), ('chan', 'sub'))]
    dynamic_update_slice x16 -> x0, local copies, waits for them, and re-layouts: 19.5 us -> none  [on_device(): peak_local, log_terms = lax.map(one_channel, (hop_rows, gap_mask))]
    ppermute x1 -> x0, waiting for transfers between devices: 14.9 us -> none  [from_behind(): return lax.ppermute(x, axis, pairs)]
    slice x9 -> x0, local copies, waits for them, and re-layouts: 10.4 us -> none  [the longest x8 9.22 us: one_channel(): segments = jnp.concatenate([rows_here[:-1], rows_here[1:]], axis=-1)]
    unnamed x1 -> x0, blocking collectives: 10 us -> none
  transfers between devices with their start and end apart: 4 -> 0, of which waited for: 4 -> 0; matrix products, arithmetic and copies ran while one was open for 3% -> 0% of each run, Pallas kernels for 0% -> 0%
where the time goes in v1:
time: 47.3 us; the launch traced here: 47.1 us
  Pallas kernels  41.9 us (89%)
  local copies, waits for them, and re-layouts  4.56 us (10%)
  between operations  0.65 us (1%)
    pallas_call x1, Pallas kernels, on_device(): pl.pallas_call(functools.partial(kernel, sizes), out_shape=[jax.ShapeDtyp...  41.9 us
    unnamed x8, local copies, waits for them, and re-layouts  4.56 us

profile of v1, /device:TPU:0, one launch (start us, length us, event | category | flops | bytes accessed | tf_op | source)
XLA Modules:
  0.0 47.1 jit_solution(3471563814258105719)
XLA Ops:
  0.6 1.3 %copy.12.gap_ref = s32[8,2]{1,0:T(8,128)} copy(s32[8,2]{0,1:T(2,128)} %param.10) | data formatting | bytes 128 | tf_op args[1]
  2.0 41.9 %shard_map.112 = (f32[8,4096]{1,0:T(8,128)}, f32[8,4096]{1,0:T(8,128)}, f32[8,4096]{1,0:T(8,128)}) custom-call(s32[8]{0:T(128)} %assign_ref.1, f32[8,32768]{1,0:T(8,128)} %x_ref.1, s32[8,2]{1,0:T(8,128)} %copy.12.gap_ref, bf16[272,256]{1,0:T(8,128)(2,1)} %constant.12.clone.one_high, bf16[272,256]{1,0:T(8,128)(2,1)} %constant.13.clone.one_low, ...), custom_call_target="tpu_custom_call" | custom-call | tf_op jit(solution)/shard_map/pallas_call | solution.py:367
  43.9 0.0 copy-start.1
  43.9 1.6 %copy.16 = f32[8,4096]{1,0:T(8,128)} copy(f32[8,4096]{1,0:T(8,128)} %get-tuple-element.6) | data formatting | bytes 262144
  45.5 0.0 copy-done.1
  45.5 0.0 copy-start
  45.5 0.7 %copy.17 = f32[8,4096]{1,0:T(8,128)} copy(f32[8,4096]{1,0:T(8,128)S(1)} %copy-done.1) | data formatting | bytes 262144
  46.2 0.3 copy-done
  46.5 0.7 %copy.18 = f32[8,4096]{1,0:T(8,128)} copy(f32[8,4096]{1,0:T(8,128)S(1)} %copy-done) | data formatting | bytes 262144
Async XLA Ops:
  43.9 1.6 %copy-start.1 = (f32[8,4096]{1,0:T(8,128)S(1)}, f32[8,4096]{1,0:T(8,128)}, u32[]{:S(2)}) copy-start(f32[8,4096]{1,0:T(8,128)} %get-tuple-element.7) | copy-start | bytes 393220
  45.5 1.0 %copy-start = (f32[8,4096]{1,0:T(8,128)S(1)}, f32[8,4096]{1,0:T(8,128)}, u32[]{:S(2)}) copy-start(f32[8,4096]{1,0:T(8,128)} %get-tuple-element.8) | copy-start | bytes 393220

commit v2 on v1

--- a/solution.py
+++ b/solution.py
@@ -117,36 +117,49 @@
             for j in range(2 * rows):
                 part = x_ref[:, j * LB : (j + 1) * LB]
                 slot, row = j // rows, j % rows
-                work[:, 2 * own + slot, row, :] = part[own * nh : (own + 1) * nh]
+                work[:, 1 + 2 * own + slot, row, :] = part[own * nh : (own + 1) * nh]
                 away[:, slot, row, :] = part[(1 - own) * nh : (2 - own) * nh]
 
-    flags = gap_ref[...].astype(F32)
+    channel_row = lax.broadcasted_iota(jnp.int32, (channels, LB), 0)
     for s in range(2):
-        masks[me, s] = jnp.broadcast_to(flags[:, s : s + 1], (channels, LB))
-
-    @pl.when(pair == pairs - 1)
-    def _():
-        work[:, 4] = jnp.zeros_like(work[:, 4])
+        flags = jnp.zeros((channels, LB), F32)
+        for c in range(channels):
+            flags = jnp.where(channel_row == c, gap_ref[s, c].astype(F32), flags)
+        masks[me, s] = flags
+
+    across = me - 1 + 2 * side
+    has_across = jnp.logical_and(across >= 0, across < times)
+
+    for own in range(2):
+        empty = 0 if own else 5
+
+        @pl.when(side == own)
+        def _():
+            work[:, empty] = jnp.zeros_like(work[:, empty])
+
+        @pl.when(jnp.logical_and(side == own, jnp.logical_not(has_across)))
+        def _():
+            work[:, 5 - empty] = jnp.zeros_like(work[:, 5 - empty])
 
     pl.semaphore_wait(barrier, times + subs + chans - 3)
 
     def raw_copy(ci):
         return pltpu.make_async_remote_copy(
             src_ref=away.at[ci],
-            dst_ref=work.at[ci, pl.ds(2 * side, 2)],
+            dst_ref=work.at[ci, pl.ds(1 + 2 * side, 2)],
             send_sem=raw_send.at[ci],
             recv_sem=raw_recv.at[ci],
             device_id={"tm": partner},
             device_id_type=MESH,
         )
 
-    def halo_copy(ci, which):
+    def halo_copy(ci):
         return pltpu.make_async_remote_copy(
-            src_ref=away.at[ci, 0] if which else work.at[ci, 0],
-            dst_ref=work.at[ci, 4],
-            send_sem=halo_send.at[which, ci],
+            src_ref=away.at[ci, side],
+            dst_ref=work.at[ci, 5 * (1 - side)],
+            send_sem=halo_send.at[ci],
             recv_sem=halo_recv.at[ci],
-            device_id={"tm": jnp.maximum(2 * pair - 2 + which, 0)},
+            device_id={"tm": lax.clamp(0, across, times - 1)},
             device_id_type=MESH,
         )
 
@@ -171,16 +184,14 @@
             device_id_type=MESH,
         )
 
-    sends_halo = jnp.logical_and(side == 0, pair > 0)
     for k in range(1, times):
         mask_copy(k).start()
     for ci in range(nh):
         raw_copy(ci).start()
 
-        @pl.when(sends_halo)
-        def _():
-            halo_copy(ci, 0).start()
-            halo_copy(ci, 1).start()
+        @pl.when(has_across)
+        def _():
+            halo_copy(ci).start()
 
     for k in range(1, times):
         source = lax.rem(me + k, times)
@@ -207,12 +218,12 @@
     def one_channel(ci, carry):
         raw_copy(ci).wait_recv()
 
-        @pl.when(pair < pairs - 1)
-        def _():
-            halo_copy(ci, 0).wait_recv()
+        @pl.when(has_across)
+        def _():
+            halo_copy(ci).wait_recv()
 
         columns_high, columns_low = [], []
-        for s in range(4):
+        for s in range(5):
             frame = jnp.concatenate(
                 [work[ci, s] * window[0], work[ci, s + 1] * window[1]], axis=0
             )
@@ -224,7 +235,7 @@
         real, imag = middle[: rows + 8], middle[rows + 8 :]
         cosine, sine = twiddle[0], twiddle[1]
         turned = []
-        for s in range(4):
+        for s in range(5):
             re, im = real[:, s * LB : (s + 1) * LB], imag[:, s * LB : (s + 1) * LB]
             turned.append(
                 jnp.concatenate([re * cosine - im * sine, re * sine + im * cosine], axis=1)
@@ -233,9 +244,13 @@
         bins = three_pass(split_value(turned), (two_high[...], two_low[...]))
         powers = bins[:, :LB] * bins[:, :LB] + bins[:, LB:] * bins[:, LB:]
         channel = side * nh + ci
+        owned = [jnp.float32(1.0)] * 5
+        owned[0] = jnp.logical_and(side == 0, has_across).astype(F32)
+        owned[4] = jnp.logical_or(side == 1, pair == pairs - 1).astype(F32)
         peak, product = None, None
-        for s in range(4):
-            keep = masks[2 * pair + s // 2, s % 2, pl.ds(channel, 1), :] > 0.5
+        for s in range(5):
+            holder = jnp.maximum(2 * pair + (s - 1) // 2, 0)
+            keep = masks[holder, (s - 1) % 2, pl.ds(channel, 1), :] * owned[s] > 0.5
             here = powers[s * (rows + 8) : (s + 1) * (rows + 8)]
             held = jnp.where(keep, here, 0.0)
             factor = jnp.where(keep, here + 0.25, 1.0)
@@ -256,23 +271,22 @@
     for t in range(times):
         kept = kept + masks[t, 0] + masks[t, 1]
 
-    for ci in range(nh):
-        for k in range(1, times):
-            source = lax.rem(me + k, times)
-            pltpu.make_async_remote_copy(
-                src_ref=arrived.at[source, ci],
-                dst_ref=arrived.at[source, ci],
-                send_sem=part_send.at[k, ci],
-                recv_sem=part_recv.at[source, ci],
-                device_id={"tm": source},
-                device_id_type=MESH,
-            ).wait_recv()
-
     count_lane = lax.broadcasted_iota(jnp.int32, (out_rows, 2 * LB), 1)
     counts = jnp.zeros((out_rows, 2 * LB), F32)
     blocks = [jnp.zeros((out_rows, 2 * LB), F32) for _ in range(BLOCKS)]
-    for c in range(channels):
+    for c in [half * nh + ci for ci in range(nh) for half in range(2)]:
         origin, ci = c // nh, c % nh
+        if origin == 0:
+            for k in range(1, times):
+                source = lax.rem(me + k, times)
+                pltpu.make_async_remote_copy(
+                    src_ref=arrived.at[source, ci],
+                    dst_ref=arrived.at[source, ci],
+                    send_sem=part_send.at[k, ci],
+                    recv_sem=part_recv.at[source, ci],
+                    device_id={"tm": source},
+                    device_id_type=MESH,
+                ).wait_recv()
         peak = arrived[origin, ci, 0]
         logs = arrived[origin, ci, 1]
         for p in range(1, pairs):
@@ -345,10 +359,9 @@
     for ci in range(nh):
         raw_copy(ci).wait_send()
 
-        @pl.when(sends_halo)
-        def _():
-            halo_copy(ci, 0).wait_send()
-            halo_copy(ci, 1).wait_send()
+        @pl.when(has_across)
+        def _():
+            halo_copy(ci).wait_send()
 
         for k in range(1, times):
             part_copy(k, ci).wait_send()
@@ -363,6 +376,7 @@
     out_rows = width // (2 * LB)
     constants = [jnp.asarray(t) for t in tables()]
     vmem = pl.BlockSpec(memory_space=pltpu.VMEM)
+    smem = pl.BlockSpec(memory_space=pltpu.SMEM)
     dma = pltpu.SemaphoreType.DMA
     return pl.pallas_call(
         functools.partial(kernel, sizes),
@@ -371,10 +385,10 @@
             jax.ShapeDtypeStruct((channels, width), F32),
             jax.ShapeDtypeStruct((BLOCKS, width), F32),
         ],
-        in_specs=[pl.BlockSpec(memory_space=pltpu.SMEM)] + [vmem] * 8,
+        in_specs=[smem, vmem, smem] + [vmem] * 6,
         out_specs=[vmem] * 3,
         scratch_shapes=[
-            pltpu.VMEM((nh, 5, rows, LB), F32),
+            pltpu.VMEM((nh, 6, rows, LB), F32),
             pltpu.VMEM((nh, 2, rows, LB), F32),
             pltpu.VMEM((times, nh, 2, out_rows, 2 * LB), F32),
             pltpu.VMEM((times, nh, 2, out_rows, 2 * LB), F32),
@@ -385,7 +399,7 @@
             pltpu.VMEM((channels, out_rows, 2 * LB), F32),
             dma((nh,)),
             dma((nh,)),
-            dma((2, nh)),
+            dma((nh,)),
             dma((nh,)),
             dma((times,)),
             dma((times,)),
@@ -397,7 +411,7 @@
             dma((chans,)),
         ],
         compiler_params=pltpu.CompilerParams(collective_id=0, has_side_effects=True),
-    )(assignment, signal, gap_mask, *constants)
+    )(assignment, signal, gap_mask.T, *constants)
 
 
 def solution(mesh):

time: 47.3 us -> 39.1 us (0.83)
  Pallas kernels: 41.9 us -> 35.1 us
  local copies, waits for them, and re-layouts: 4.56 us -> 3.21 us
    pallas_call x1, Pallas kernels: 41.9 us -> 35.1 us  [on_device(): pl.pallas_call(functools.partial(kernel, sizes), out_shape=[jax.ShapeDtyp...]
    unnamed x8 -> x7, local copies, waits for them, and re-layouts: 4.56 us -> 3.21 us
where the time goes in v2:
time: 39.1 us; the launch traced here: 38.9 us
  Pallas kernels  35.1 us (90%)
  local copies, waits for them, and re-layouts  3.21 us (8%)
  between operations  0.65 us (2%)
    pallas_call x1, Pallas kernels, on_device(): pl.pallas_call(functools.partial(kernel, sizes), out_shape=[jax.ShapeDtyp...  35.1 us
    unnamed x7, local copies, waits for them, and re-layouts  3.21 us

profile of v2, /device:TPU:0, one launch (start us, length us, event | category | flops | bytes accessed | tf_op | source)
XLA Modules:
  0.0 38.9 jit_solution(422640112070154491)
XLA Ops:
  0.6 35.1 %shard_map.112 = (f32[8,4096]{1,0:T(8,128)}, f32[8,4096]{1,0:T(8,128)}, f32[8,4096]{1,0:T(8,128)}) custom-call(s32[8]{0:T(128)} %assign_ref.1, f32[8,32768]{1,0:T(8,128)} %x_ref.1, s32[2,8]{1,0:T(2,128)} %bitcast.1, bf16[272,256]{1,0:T(8,128)(2,1)} %constant.12.clone.one_high, bf16[272,256]{1,0:T(8,128)(2,1)} %constant.13.clone.one_low, ...), custom_call_target="tpu_custom_call" | custom-call | tf_op jit(solution)/shard_map/pallas_call | solution.py:381
  35.7 0.0 copy-start.1
  35.7 1.6 %copy.15 = f32[8,4096]{1,0:T(8,128)} copy(f32[8,4096]{1,0:T(8,128)} %get-tuple-element.6) | data formatting | bytes 262144
  37.3 0.0 copy-done.1
  37.3 0.0 copy-start
  37.3 0.7 %copy.16 = f32[8,4096]{1,0:T(8,128)} copy(f32[8,4096]{1,0:T(8,128)S(1)} %copy-done.1) | data formatting | bytes 262144
  38.0 0.3 copy-done
  38.3 0.7 %copy.17 = f32[8,4096]{1,0:T(8,128)} copy(f32[8,4096]{1,0:T(8,128)S(1)} %copy-done) | data formatting | bytes 262144
Async XLA Ops:
  35.7 1.6 %copy-start.1 = (f32[8,4096]{1,0:T(8,128)S(1)}, f32[8,4096]{1,0:T(8,128)}, u32[]{:S(2)}) copy-start(f32[8,4096]{1,0:T(8,128)} %get-tuple-element.7) | copy-start | bytes 393220
  37.3 1.0 %copy-start = (f32[8,4096]{1,0:T(8,128)S(1)}, f32[8,4096]{1,0:T(8,128)}, u32[]{:S(2)}) copy-start(f32[8,4096]{1,0:T(8,128)} %get-tuple-element.8) | copy-start | bytes 393220

commit v3 on v2

--- a/solution.py
+++ b/solution.py
@@ -58,26 +58,23 @@
 def kernel(
     sizes,
     assign_ref,
-    x_ref,
+    x_in,
     gap_ref,
-    one_high,
-    one_low,
-    two_high,
-    two_low,
-    twiddle,
-    window,
-    peak_out,
-    mean_out,
-    block_out,
+    *refs,
+):
+    inputs = (x_in, *refs[:6])
+    peak_out, mean_out, block_out = refs[6:9]
+    local = refs[9:16]
+    x_ref, one_high, one_low, two_high, two_low, twiddle, window = local
+    (
     work,
     away,
     stage,
     arrived,
     masks,
-    sub_sums,
-    chan_sums,
-    peak_rows,
-    mean_rows,
+    means,
+    owners,
+    local_sem,
     raw_send,
     raw_recv,
     halo_send,
@@ -86,30 +83,41 @@
     mask_recv,
     part_send,
     part_recv,
-    sub_send,
-    sub_recv,
-    chan_send,
-    chan_recv,
-):
+    mean_send,
+    mean_recv,
+    owner_send,
+    owner_recv,
+    ) = refs[16:]
     times, subs, chans = sizes
     pairs = times // 2
     channels = x_ref.shape[0]
     nh = channels // 2
     rows = LA // 2
     out_rows = stage.shape[3]
+    peers = subs * chans
     me = lax.axis_index("tm")
     pair, side = me // 2, lax.rem(me, 2)
     partner = pair * 2 + 1 - side
     my_sub = lax.axis_index("sub")
     my_chan = lax.axis_index("chan")
+    mine = my_chan * subs + my_sub
+    copies = [pltpu.make_async_copy(a, b, local_sem.at[i]) for i, (a, b) in enumerate(zip(inputs, local))]
+    for one in copies:
+        one.start()
+
+    def peer(k):
+        other = lax.rem(mine + k, peers)
+        return {"chan": other // subs, "sub": lax.rem(other, subs)}
 
     barrier = pltpu.get_barrier_semaphore()
-    for axis, here, count in (("tm", me, times), ("sub", my_sub, subs), ("chan", my_chan, chans)):
-        for k in range(1, count):
-            pl.semaphore_signal(
-                barrier, inc=1, device_id={axis: lax.rem(here + k, count)}, device_id_type=MESH
-            )
-
+    for k in range(1, times):
+        pl.semaphore_signal(
+            barrier, inc=1, device_id={"tm": lax.rem(me + k, times)}, device_id_type=MESH
+        )
+    for k in range(1, peers):
+        pl.semaphore_signal(barrier, inc=1, device_id=peer(k), device_id_type=MESH)
+
+    copies[0].wait()
     for own in range(2):
 
         @pl.when(side == own)
@@ -127,6 +135,11 @@
             flags = jnp.where(channel_row == c, gap_ref[s, c].astype(F32), flags)
         masks[me, s] = flags
 
+    owner = jnp.zeros((channels, LB), jnp.int32)
+    for c in range(channels):
+        owner = jnp.where(channel_row == c, assign_ref[c], owner)
+    owners[mine] = owner.astype(F32)
+
     across = me - 1 + 2 * side
     has_across = jnp.logical_and(across >= 0, across < times)
 
@@ -141,7 +154,7 @@
         def _():
             work[:, 5 - empty] = jnp.zeros_like(work[:, 5 - empty])
 
-    pl.semaphore_wait(barrier, times + subs + chans - 3)
+    pl.semaphore_wait(barrier, times + peers - 2)
 
     def raw_copy(ci):
         return pltpu.make_async_remote_copy(
@@ -173,8 +186,30 @@
             device_id_type=MESH,
         )
 
+    def owner_copy(k, slot):
+        return pltpu.make_async_remote_copy(
+            src_ref=owners.at[slot],
+            dst_ref=owners.at[slot],
+            send_sem=owner_send.at[k],
+            recv_sem=owner_recv.at[slot],
+            device_id=peer(k),
+            device_id_type=MESH,
+        )
+
+    def mean_copy(k, slot, ci):
+        return pltpu.make_async_remote_copy(
+            src_ref=means.at[slot, ci],
+            dst_ref=means.at[slot, ci],
+            send_sem=mean_send.at[k, ci],
+            recv_sem=mean_recv.at[slot, ci],
+            device_id=peer(k),
+            device_id_type=MESH,
+        )
+
+    toward = jnp.where(2 * me < times, times - 1, 1)
+
     def part_copy(k, ci):
-        target = lax.rem(me + k, times)
+        target = lax.rem(me + k * toward, times)
         return pltpu.make_async_remote_copy(
             src_ref=stage.at[target, ci],
             dst_ref=arrived.at[me, ci],
@@ -186,6 +221,8 @@
 
     for k in range(1, times):
         mask_copy(k).start()
+    for k in range(1, peers):
+        owner_copy(k, mine).start()
     for ci in range(nh):
         raw_copy(ci).start()
 
@@ -203,6 +240,11 @@
             device_id={"tm": source},
             device_id_type=MESH,
         ).wait_recv()
+
+    for k in range(1, peers):
+        owner_copy(k, lax.rem(mine + k, peers)).wait_recv()
+    for one in copies[1:]:
+        one.wait()
 
     lane = lax.broadcasted_iota(jnp.int32, (8, LB), 1)
     sub_row = lax.broadcasted_iota(jnp.int32, (8, LB), 0)
@@ -271,89 +313,64 @@
     for t in range(times):
         kept = kept + masks[t, 0] + masks[t, 1]
 
-    count_lane = lax.broadcasted_iota(jnp.int32, (out_rows, 2 * LB), 1)
-    counts = jnp.zeros((out_rows, 2 * LB), F32)
     blocks = [jnp.zeros((out_rows, 2 * LB), F32) for _ in range(BLOCKS)]
-    for c in [half * nh + ci for ci in range(nh) for half in range(2)]:
-        origin, ci = c // nh, c % nh
-        if origin == 0:
-            for k in range(1, times):
-                source = lax.rem(me + k, times)
-                pltpu.make_async_remote_copy(
-                    src_ref=arrived.at[source, ci],
-                    dst_ref=arrived.at[source, ci],
-                    send_sem=part_send.at[k, ci],
-                    recv_sem=part_recv.at[source, ci],
-                    device_id={"tm": source},
-                    device_id_type=MESH,
-                ).wait_recv()
-        peak = arrived[origin, ci, 0]
-        logs = arrived[origin, ci, 1]
-        for p in range(1, pairs):
-            peak = jnp.maximum(peak, arrived[2 * p + origin, ci, 0])
-            logs = logs + arrived[2 * p + origin, ci, 1]
-        row = kept[c : c + 1]
-        mean = logs / jnp.concatenate([row, row], axis=1)
-        peak_rows[c] = peak
-        mean_rows[c] = mean
-        group = assign_ref[c]
-        counts = counts + (count_lane == group).astype(F32)
-        for b in range(BLOCKS):
-            blocks[b] = blocks[b] + mean * (group == b).astype(F32)
+
+    def add_means(blocks, slot, ci):
+        for half in range(2):
+            mean = means[slot, ci, half]
+            row = owners[slot, half * nh + ci : half * nh + ci + 1, :]
+            row = jnp.concatenate([row, row], axis=1)
+            blocks = [total + mean * (row == b).astype(F32) for b, total in enumerate(blocks)]
+        return blocks
+
+    for ci in range(nh):
+        for k in range(1, times):
+            source = lax.rem(me + k, times)
+            pltpu.make_async_remote_copy(
+                src_ref=arrived.at[source, ci],
+                dst_ref=arrived.at[source, ci],
+                send_sem=part_send.at[k, ci],
+                recv_sem=part_recv.at[source, ci],
+                device_id={"tm": source},
+                device_id_type=MESH,
+            ).wait_recv()
+        for half in range(2):
+            c = half * nh + ci
+            peak = arrived[half, ci, 0]
+            logs = arrived[half, ci, 1]
+            for p in range(1, pairs):
+                peak = jnp.maximum(peak, arrived[2 * p + half, ci, 0])
+                logs = logs + arrived[2 * p + half, ci, 1]
+            row = kept[c : c + 1]
+            mean = logs / jnp.concatenate([row, row], axis=1)
+            peak_out[c] = peak
+            mean_out[c] = mean
+            means[mine, ci, half] = mean
+        for k in range(1, peers):
+            mean_copy(k, mine, ci).start()
+        if ci > 0:
+            for k in range(1, peers):
+                mean_copy(k, lax.rem(mine + k, peers), ci - 1).wait_recv()
+            for slot in range(peers):
+                blocks = add_means(blocks, slot, ci - 1)
+    sizes_of = []
     for b in range(BLOCKS):
-        sub_sums[my_sub, b] = blocks[b]
-    sub_sums[my_sub, BLOCKS] = counts
-
-    def exchange(axis, here, count, sums, send, recv):
-        def copy(k, owner):
-            return pltpu.make_async_remote_copy(
-                src_ref=sums.at[owner],
-                dst_ref=sums.at[owner],
-                send_sem=send.at[k],
-                recv_sem=recv.at[owner],
-                device_id={axis: lax.rem(here + k, count)},
-                device_id_type=MESH,
-            )
-
-        sends = [copy(k, here) for k in range(1, count)]
-        for one in sends:
-            one.start()
-        return sends, [copy(k, lax.rem(here + k, count)) for k in range(1, count)]
-
-    sub_out, sub_in = exchange("sub", my_sub, subs, sub_sums, sub_send, sub_recv)
-    for j in range(out_rows):
-        for side_lane in range(2):
-            at = (2 * j + side_lane) * LB
-            lanes = slice(side_lane * LB, (side_lane + 1) * LB)
-            peak_out[:, at : at + LB] = peak_rows[:, j, lanes]
-            mean_out[:, at : at + LB] = mean_rows[:, j, lanes]
-    for one in sub_in:
-        one.wait_recv()
-    for b in range(BLOCKS + 1):
-        total = sub_sums[0, b]
-        for k in range(1, subs):
-            total = total + sub_sums[k, b]
-        chan_sums[my_chan, b] = total
-    chan_out, chan_in = exchange("chan", my_chan, chans, chan_sums, chan_send, chan_recv)
-    for one in chan_in:
-        one.wait_recv()
-    totals = []
-    for b in range(BLOCKS + 1):
-        total = chan_sums[0, b]
-        for k in range(1, chans):
-            total = total + chan_sums[k, b]
-        totals.append(total)
+        held = jnp.zeros((channels, LB), F32)
+        for slot in range(peers):
+            held = held + (owners[slot] == b).astype(F32)
+        size = jnp.sum(held, axis=0, keepdims=True)
+        sizes_of.append(jnp.concatenate([size, size], axis=1))
+    for k in range(1, peers):
+        mean_copy(k, lax.rem(mine + k, peers), nh - 1).wait_recv()
+    for slot in range(peers):
+        blocks = add_means(blocks, slot, nh - 1)
     for b in range(BLOCKS):
-        size = jnp.sum(jnp.where(count_lane == b, totals[BLOCKS], 0.0), axis=1, keepdims=True)
-        peak_rows[b] = totals[b] / size
-    for j in range(out_rows):
-        for side_lane in range(2):
-            at = (2 * j + side_lane) * LB
-            lanes = slice(side_lane * LB, (side_lane + 1) * LB)
-            block_out[:, at : at + LB] = peak_rows[:BLOCKS, j, lanes]
-
-    for one in sub_out + chan_out:
-        one.wait_send()
+        block_out[b] = blocks[b] / sizes_of[b]
+
+    for k in range(1, peers):
+        owner_copy(k, mine).wait_send()
+        for ci in range(nh):
+            mean_copy(k, mine, ci).wait_send()
     for k in range(1, times):
         mask_copy(k).wait_send()
     for ci in range(nh):
@@ -365,6 +382,14 @@
 
         for k in range(1, times):
             part_copy(k, ci).wait_send()
+
+
+def flatten(*refs):
+    for lines, flat in zip(refs[:3], refs[3:]):
+        for j in range(lines.shape[1]):
+            for half in range(2):
+                at = (2 * j + half) * LB
+                flat[:, at : at + LB] = lines[:, j, half * LB : (half + 1) * LB]
 
 
 def on_device(sizes, signal, gap_mask, assignment):
@@ -374,29 +399,29 @@
     rows = LA // 2
     width = LA * LB // 2 // times
     out_rows = width // (2 * LB)
+    peers = subs * chans
     constants = [jnp.asarray(t) for t in tables()]
     vmem = pl.BlockSpec(memory_space=pltpu.VMEM)
     smem = pl.BlockSpec(memory_space=pltpu.SMEM)
+    hbm = pl.BlockSpec(memory_space=pl.ANY)
     dma = pltpu.SemaphoreType.DMA
-    return pl.pallas_call(
+    inputs = [signal, *constants]
+    lines = [(channels, out_rows, 2 * LB)] * 2 + [(BLOCKS, out_rows, 2 * LB)]
+    found = pl.pallas_call(
         functools.partial(kernel, sizes),
-        out_shape=[
-            jax.ShapeDtypeStruct((channels, width), F32),
-            jax.ShapeDtypeStruct((channels, width), F32),
-            jax.ShapeDtypeStruct((BLOCKS, width), F32),
-        ],
-        in_specs=[smem, vmem, smem] + [vmem] * 6,
+        out_shape=[jax.ShapeDtypeStruct(shape, F32) for shape in lines],
+        in_specs=[smem, hbm, smem] + [hbm] * 6,
         out_specs=[vmem] * 3,
         scratch_shapes=[
+            *[pltpu.VMEM(one.shape, one.dtype) for one in inputs],
             pltpu.VMEM((nh, 6, rows, LB), F32),
             pltpu.VMEM((nh, 2, rows, LB), F32),
             pltpu.VMEM((times, nh, 2, out_rows, 2 * LB), F32),
             pltpu.VMEM((times, nh, 2, out_rows, 2 * LB), F32),
             pltpu.VMEM((times, 2, channels, LB), F32),
-            pltpu.VMEM((subs, BLOCKS + 1, out_rows, 2 * LB), F32),
-            pltpu.VMEM((chans, BLOCKS + 1, out_rows, 2 * LB), F32),
-            pltpu.VMEM((max(channels, BLOCKS), out_rows, 2 * LB), F32),
-            pltpu.VMEM((channels, out_rows, 2 * LB), F32),
+            pltpu.VMEM((peers, nh, 2, out_rows, 2 * LB), F32),
+            pltpu.VMEM((peers, channels, LB), F32),
+            dma((len(inputs),)),
             dma((nh,)),
             dma((nh,)),
             dma((nh,)),
@@ -405,13 +430,19 @@
             dma((times,)),
             dma((times, nh)),
             dma((times, nh)),
-            dma((subs,)),
-            dma((subs,)),
-            dma((chans,)),
-            dma((chans,)),
+            dma((peers, nh)),
+            dma((peers, nh)),
+            dma((peers,)),
+            dma((peers,)),
         ],
         compiler_params=pltpu.CompilerParams(collective_id=0, has_side_effects=True),
     )(assignment, signal, gap_mask.T, *constants)
+    return pl.pallas_call(
+        flatten,
+        out_shape=[jax.ShapeDtypeStruct((shape[0], width), F32) for shape in lines],
+        in_specs=[vmem] * 3,
+        out_specs=[vmem] * 3,
+    )(*found)
 
 
 def solution(mesh):

time: 39.1 us -> 36.8 us (0.941)
  local copies, waits for them, and re-layouts: 3.21 us -> 0 us
  Pallas kernels: 35.1 us -> 35.9 us
    unnamed x7 -> x0, local copies, waits for them, and re-layouts: 3.21 us -> none
    pallas_call x0 -> x1, Pallas kernels: none -> 1.92 us  [on_device(): pl.pallas_call(flatten, out_shape=[jax.ShapeDtypeStruct((shape[0], width)...]
    pallas_call x1, Pallas kernels: 35.1 us -> 34 us  [on_device(): pl.pallas_call(functools.partial(kernel, sizes), out_shape=[jax.ShapeDtyp...]
where the time goes in v3:
time: 36.8 us; the launch traced here: 36.6 us
  Pallas kernels  35.9 us (98%)
  between operations  0.64 us (2%)
    pallas_call x1, Pallas kernels, on_device(): pl.pallas_call(functools.partial(kernel, sizes), out_shape=[jax.ShapeDtyp...  34 us
    pallas_call x1, Pallas kernels, on_device(): pl.pallas_call(flatten, out_shape=[jax.ShapeDtypeStruct((shape[0], width)...  1.92 us

profile of v3, /device:TPU:0, one launch (start us, length us, event | category | flops | bytes accessed | tf_op | source)
XLA Modules:
  0.0 36.6 jit_solution(2009317258720388979)
XLA Ops:
  0.6 34.0 %shard_map.112 = (f32[8,16,256]{2,1,0:T(8,128)}, f32[8,16,256]{2,1,0:T(8,128)}, f32[8,16,256]{2,1,0:T(8,128)}) custom-call(s32[8]{0:T(128)} %assign_ref.1, f32[8,32768]{1,0:T(8,128)} %x_in.1, s32[2,8]{1,0:T(2,128)} %bitcast.1, bf16[272,256]{1,0:T(8,128)(2,1)} %constant.12.clone.refs_0_, bf16[272,256]{1,0:T(8,128)(2,1)} %constant.13.clone.refs_1_, ...), custom_call_target="tpu_custom_call" | custom-call | tf_op jit(solution)/shard_map/pallas_call | solution.py:410
  34.7 1.9 %shard_map.113 = (f32[8,4096]{1,0:T(8,128)}, f32[8,4096]{1,0:T(8,128)}, f32[8,4096]{1,0:T(8,128)}) custom-call(f32[8,16,256]{2,1,0:T(8,128)} %get-tuple-element.6.refs_0_, f32[8,16,256]{2,1,0:T(8,128)} %get-tuple-element.7.refs_1_, f32[8,16,256]{2,1,0:T(8,128)} %get-tuple-element.8.refs_2_), custom_call_target="tpu_custom_call" | custom-call | tf_op jit(solution)/shard_map/pallas_call | solution.py:440

commit v4 on v3

--- a/solution.py
+++ b/solution.py
@@ -208,13 +208,13 @@
 
     toward = jnp.where(2 * me < times, times - 1, 1)
 
-    def part_copy(k, ci):
+    def part_copy(k, ci, which):
         target = lax.rem(me + k * toward, times)
         return pltpu.make_async_remote_copy(
-            src_ref=stage.at[target, ci],
-            dst_ref=arrived.at[me, ci],
-            send_sem=part_send.at[k, ci],
-            recv_sem=part_recv.at[me, ci],
+            src_ref=stage.at[target, ci, which],
+            dst_ref=arrived.at[me, ci, which],
+            send_sem=part_send.at[k, ci, which],
+            recv_sem=part_recv.at[me, ci, which],
             device_id={"tm": target},
             device_id_type=MESH,
         )
@@ -303,11 +303,14 @@
             for target in range(times):
                 stage[target, ci, which] = ordered[target * out_rows : (target + 1) * out_rows]
         for k in range(1, times):
-            part_copy(k, ci).start()
+            part_copy(k, ci, 1).start()
         arrived[me, ci] = stage[me, ci]
         return carry
 
     lax.fori_loop(0, nh, one_channel, 0)
+    for ci in range(nh):
+        for k in range(1, times):
+            part_copy(k, ci, 0).start()
 
     kept = jnp.zeros((channels, LB), F32)
     for t in range(times):
@@ -323,27 +326,27 @@
             blocks = [total + mean * (row == b).astype(F32) for b, total in enumerate(blocks)]
         return blocks
 
-    for ci in range(nh):
+    def await_parts(ci, which):
         for k in range(1, times):
             source = lax.rem(me + k, times)
             pltpu.make_async_remote_copy(
-                src_ref=arrived.at[source, ci],
-                dst_ref=arrived.at[source, ci],
-                send_sem=part_send.at[k, ci],
-                recv_sem=part_recv.at[source, ci],
+                src_ref=arrived.at[source, ci, which],
+                dst_ref=arrived.at[source, ci, which],
+                send_sem=part_send.at[k, ci, which],
+                recv_sem=part_recv.at[source, ci, which],
                 device_id={"tm": source},
                 device_id_type=MESH,
             ).wait_recv()
+
+    for ci in range(nh):
+        await_parts(ci, 1)
         for half in range(2):
             c = half * nh + ci
-            peak = arrived[half, ci, 0]
             logs = arrived[half, ci, 1]
             for p in range(1, pairs):
-                peak = jnp.maximum(peak, arrived[2 * p + half, ci, 0])
                 logs = logs + arrived[2 * p + half, ci, 1]
             row = kept[c : c + 1]
             mean = logs / jnp.concatenate([row, row], axis=1)
-            peak_out[c] = peak
             mean_out[c] = mean
             means[mine, ci, half] = mean
         for k in range(1, peers):
@@ -353,6 +356,13 @@
                 mean_copy(k, lax.rem(mine + k, peers), ci - 1).wait_recv()
             for slot in range(peers):
                 blocks = add_means(blocks, slot, ci - 1)
+    for ci in range(nh):
+        await_parts(ci, 0)
+        for half in range(2):
+            peak = arrived[half, ci, 0]
+            for p in range(1, pairs):
+                peak = jnp.maximum(peak, arrived[2 * p + half, ci, 0])
+            peak_out[half * nh + ci] = peak
     sizes_of = []
     for b in range(BLOCKS):
         held = jnp.zeros((channels, LB), F32)
@@ -381,7 +391,8 @@
             halo_copy(ci).wait_send()
 
         for k in range(1, times):
-            part_copy(k, ci).wait_send()
+            for which in range(2):
+                part_copy(k, ci, which).wait_send()
 
 
 def flatten(*refs):
@@ -428,8 +439,8 @@
             dma((nh,)),
             dma((times,)),
             dma((times,)),
-            dma((times, nh)),
-            dma((times, nh)),
+            dma((times, nh, 2)),
+            dma((times, nh, 2)),
             dma((peers, nh)),
             dma((peers, nh)),
             dma((peers,)),

time: 36.8 us -> 34.7 us (0.943)
  Pallas kernels: 35.9 us -> 33.9 us
    pallas_call x1, Pallas kernels: 34 us -> 31.9 us  [on_device(): pl.pallas_call(functools.partial(kernel, sizes), out_shape=[jax.ShapeDtyp...]
where the time goes in v4:
time: 34.7 us; the launch traced here: 34.5 us
  Pallas kernels  33.9 us (98%)
  between operations  0.64 us (2%)
    pallas_call x1, Pallas kernels, on_device(): pl.pallas_call(functools.partial(kernel, sizes), out_shape=[jax.ShapeDtyp...  31.9 us
    pallas_call x1, Pallas kernels, on_device(): pl.pallas_call(flatten, out_shape=[jax.ShapeDtypeStruct((shape[0], width)...  1.92 us

profile of v4, /device:TPU:0, one launch (start us, length us, event | category | flops | bytes accessed | tf_op | source)
XLA Modules:
  0.0 34.5 jit_solution(12902834614643414353)
XLA Ops:
  0.6 31.9 %shard_map.112 = (f32[8,16,256]{2,1,0:T(8,128)}, f32[8,16,256]{2,1,0:T(8,128)}, f32[8,16,256]{2,1,0:T(8,128)}) custom-call(s32[8]{0:T(128)} %assign_ref.1, f32[8,32768]{1,0:T(8,128)} %x_in.1, s32[2,8]{1,0:T(2,128)} %bitcast.1, bf16[272,256]{1,0:T(8,128)(2,1)} %constant.12.clone.refs_0_, bf16[272,256]{1,0:T(8,128)(2,1)} %constant.13.clone.refs_1_, ...), custom_call_target="tpu_custom_call" | custom-call | tf_op jit(solution)/shard_map/pallas_call | solution.py:421
  32.6 1.9 %shard_map.113 = (f32[8,4096]{1,0:T(8,128)}, f32[8,4096]{1,0:T(8,128)}, f32[8,4096]{1,0:T(8,128)}) custom-call(f32[8,16,256]{2,1,0:T(8,128)} %get-tuple-element.6.refs_0_, f32[8,16,256]{2,1,0:T(8,128)} %get-tuple-element.7.refs_1_, f32[8,16,256]{2,1,0:T(8,128)} %get-tuple-element.8.refs_2_), custom_call_target="tpu_custom_call" | custom-call | tf_op jit(solution)/shard_map/pallas_call | solution.py:451

commit v5 on v4

--- a/solution.py
+++ b/solution.py
@@ -420,7 +420,7 @@
     lines = [(channels, out_rows, 2 * LB)] * 2 + [(BLOCKS, out_rows, 2 * LB)]
     found = pl.pallas_call(
         functools.partial(kernel, sizes),
-        out_shape=[jax.ShapeDtypeStruct(shape, F32) for shape in lines],
+        out_shape=[pltpu.VMEM(shape, F32) for shape in lines],
         in_specs=[smem, hbm, smem] + [hbm] * 6,
         out_specs=[vmem] * 3,
         scratch_shapes=[
@@ -453,7 +453,7 @@
         out_shape=[jax.ShapeDtypeStruct((shape[0], width), F32) for shape in lines],
         in_specs=[vmem] * 3,
         out_specs=[vmem] * 3,
-    )(*found)
+    )(*[pltpu.with_memory_space_constraint(one, pltpu.VMEM) for one in found])
 
 
 def solution(mesh):

time: 34.7 us -> 32.9 us (0.948)
  Pallas kernels: 33.9 us -> 32.1 us
    pallas_call x1, Pallas kernels: 1.92 us -> 0.9 us  [on_device(): pl.pallas_call(flatten, out_shape=[jax.ShapeDtypeStruct((shape[0], width)...]
    pallas_call x1, Pallas kernels: 31.9 us -> 31.2 us  [on_device(): pl.pallas_call(functools.partial(kernel, sizes), out_shape=[pltpu.VMEM(sh...]
where the time goes in v5:
time: 32.9 us; the launch traced here: 32.7 us
  Pallas kernels  32.1 us (98%)
  between operations  0.64 us (2%)
    pallas_call x1, Pallas kernels, on_device(): pl.pallas_call(functools.partial(kernel, sizes), out_shape=[pltpu.VMEM(sh...  31.2 us
    pallas_call x1, Pallas kernels, on_device(): pl.pallas_call(flatten, out_shape=[jax.ShapeDtypeStruct((shape[0], width)...  0.9 us

profile of v5, /device:TPU:0, one launch (start us, length us, event | category | flops | bytes accessed | tf_op | source)
XLA Modules:
  0.0 32.7 jit_solution(6895608495995263072)
XLA Ops:
  0.6 31.2 %shard_map.112 = (f32[8,16,256]{2,1,0:T(8,128)S(1)}, f32[8,16,256]{2,1,0:T(8,128)S(1)}, f32[8,16,256]{2,1,0:T(8,128)S(1)}) custom-call(s32[8]{0:T(128)} %assign_ref.1, f32[8,32768]{1,0:T(8,128)} %x_in.1, s32[2,8]{1,0:T(2,128)} %bitcast.1, bf16[272,256]{1,0:T(8,128)(2,1)} %constant.12.clone.refs_0_, bf16[272,256]{1,0:T(8,128)(2,1)} %constant.13.clone.refs_1_, ...), custom_call_target="tpu_custom_call" | custom-call | tf_op jit(solution)/shard_map/pallas_call | solution.py:421
  31.8 0.9 %shard_map.113 = (f32[8,4096]{1,0:T(8,128)}, f32[8,4096]{1,0:T(8,128)}, f32[8,4096]{1,0:T(8,128)}) custom-call(f32[8,16,256]{2,1,0:T(8,128)S(1)} %get-tuple-element.6.refs_0_, f32[8,16,256]{2,1,0:T(8,128)S(1)} %get-tuple-element.7.refs_1_, f32[8,16,256]{2,1,0:T(8,128)S(1)} %get-tuple-element.8.refs_2_), custom_call_target="tpu_custom_call" | custom-call | tf_op jit(solution)/shard_map/pallas_call | solution.py:451

commit v6 on v5

--- a/solution.py
+++ b/solution.py
@@ -308,8 +308,8 @@
         return carry
 
     lax.fori_loop(0, nh, one_channel, 0)
-    for ci in range(nh):
-        for k in range(1, times):
+    for k in range(1, times):
+        for ci in range(nh):
             part_copy(k, ci, 0).start()
 
     kept = jnp.zeros((channels, LB), F32)

time: 32.9 us -> 32.4 us (0.985)
  Pallas kernels: 32.1 us -> 31.6 us
    pallas_call x1, Pallas kernels: 31.2 us -> 30.7 us  [on_device(): pl.pallas_call(functools.partial(kernel, sizes), out_shape=[pltpu.VMEM(sh...]
where the time goes in v6:
time: 32.4 us; the launch traced here: 32.2 us
  Pallas kernels  31.6 us (98%)
  between operations  0.64 us (2%)
    pallas_call x1, Pallas kernels, on_device(): pl.pallas_call(functools.partial(kernel, sizes), out_shape=[pltpu.VMEM(sh...  30.7 us
    pallas_call x1, Pallas kernels, on_device(): pl.pallas_call(flatten, out_shape=[jax.ShapeDtypeStruct((shape[0], width)...  0.9 us

profile of v6, /device:TPU:0, one launch (start us, length us, event | category | flops | bytes accessed | tf_op | source)
XLA Modules:
  0.0 32.2 jit_solution(1528248745389759628)
XLA Ops:
  0.6 30.7 %shard_map.112 = (f32[8,16,256]{2,1,0:T(8,128)S(1)}, f32[8,16,256]{2,1,0:T(8,128)S(1)}, f32[8,16,256]{2,1,0:T(8,128)S(1)}) custom-call(s32[8]{0:T(128)} %assign_ref.1, f32[8,32768]{1,0:T(8,128)} %x_in.1, s32[2,8]{1,0:T(2,128)} %bitcast.1, bf16[272,256]{1,0:T(8,128)(2,1)} %constant.12.clone.refs_0_, bf16[272,256]{1,0:T(8,128)(2,1)} %constant.13.clone.refs_1_, ...), custom_call_target="tpu_custom_call" | custom-call | tf_op jit(solution)/shard_map/pallas_call | solution.py:421
  31.3 0.9 %shard_map.113 = (f32[8,4096]{1,0:T(8,128)}, f32[8,4096]{1,0:T(8,128)}, f32[8,4096]{1,0:T(8,128)}) custom-call(f32[8,16,256]{2,1,0:T(8,128)S(1)} %get-tuple-element.6.refs_0_, f32[8,16,256]{2,1,0:T(8,128)S(1)} %get-tuple-element.7.refs_1_, f32[8,16,256]{2,1,0:T(8,128)S(1)} %get-tuple-element.8.refs_2_), custom_call_target="tpu_custom_call" | custom-call | tf_op jit(solution)/shard_map/pallas_call | solution.py:451
